TPU v7x, 32 devices: a whole 2x2x4 slice. The times are simulated.
32 devices in a mesh: row: 4 (over z), col: 8 (over y, x, core).
Axes of the slice: x: 2, y: 2, z: 4, core: 2. Of those that a mesh axis runs over, the one named last changes fastest.
Arguments:
- tokens: bfloat16 [1024, 8192], P('row', 'col'), may hold values from -6 to 6
- gate_frozen_weight: bfloat16 [8192, 28672], P('col', 'row'), may hold values from -0.0625 to 0.0625
- gate_left_factor: bfloat16 [8192, 64], P('col'), may hold values from -0.046875 to 0.046875
- gate_right_factor: bfloat16 [64, 28672], P(None, 'row'), may hold values from -0.75 to 0.75
- gate_column_magnitude: float32 [28672], P('row'), may hold values from 0.5 to 1.5
- up_frozen_weight: bfloat16 [8192, 28672], P('col', 'row'), may hold values from -0.0625 to 0.0625
- up_left_factor: bfloat16 [8192, 64], P('col'), may hold values from -0.046875 to 0.046875
- up_right_factor: bfloat16 [64, 28672], P(None, 'row'), may hold values from -0.75 to 0.75
- up_column_magnitude: float32 [28672], P('row'), may hold values from 0.5 to 1.5
- down_frozen_weight: bfloat16 [28672, 8192], P('row', 'col'), may hold values from -0.03125 to 0.03125
- down_left_factor: bfloat16 [28672, 64], P('row'), may hold values from -0.02734375 to 0.02734375
- down_right_factor: bfloat16 [64, 8192], P(None, 'col'), may hold values from -0.75 to 0.75
- down_column_magnitude: float32 [8192], P('col'), may hold values from 0.5 to 1.5
Outputs:
- mixed: bfloat16 [1024, 8192], P('row', 'col')
All inputs are finite; a program needn't handle non-finite values.
Results may differ from a plain program's by a relative error of at most 0.028.
Values may be sent and summed in bfloat16 or wider, within the bound.
A program may use at most 192 MiB of HBM per device.

v0:
```python
import jax
import jax.numpy as jnp
from jax import lax
from jax.sharding import PartitionSpec as P

stability_offset = 1e-06


def column_square_totals(weight, low_b, low_a):
    merged = weight.astype(jnp.float32) + jnp.dot(low_b, low_a, preferred_element_type=jnp.float32)
    return jnp.sum(merged * merged, axis=0)


def plain_term(inputs, weight):
    return jnp.dot(inputs, weight, preferred_element_type=jnp.float32)


def rank_update_term(inputs, weight, low_b, low_a):
    value = jnp.dot(inputs, weight, preferred_element_type=jnp.float32)
    coords = jnp.dot(inputs, low_b, preferred_element_type=jnp.float32)
    return value + jnp.dot(coords, low_a.astype(jnp.float32), precision=lax.Precision.HIGHEST)


def shards(
    tokens,
    gate_frozen_weight,
    gate_left_factor,
    gate_right_factor,
    gate_column_magnitude,
    up_frozen_weight,
    up_left_factor,
    up_right_factor,
    up_column_magnitude,
    down_frozen_weight,
    down_left_factor,
    down_right_factor,
    down_column_magnitude,
):
    token_rows_full = lax.all_gather(tokens, "row", axis=0, tiled=True)
    gate_sq, up_sq = lax.psum(
        (
            column_square_totals(gate_frozen_weight, gate_left_factor, gate_right_factor),
            column_square_totals(up_frozen_weight, up_left_factor, up_right_factor),
        ),
        "col",
    )
    down_squared = lax.psum(
        column_square_totals(down_frozen_weight, down_left_factor, down_right_factor), "row"
    )
    gate_column_scale = gate_column_magnitude / jnp.sqrt(gate_sq + stability_offset)
    up_column_scale = up_column_magnitude / jnp.sqrt(up_sq + stability_offset)
    down_column_scale = down_column_magnitude / jnp.sqrt(down_squared + stability_offset)
    own_count = token_rows_full.shape[0] // lax.axis_size("col")
    gate_coordinate_slice = jnp.dot(
        token_rows_full, gate_left_factor, preferred_element_type=jnp.float32
    )
    up_coordinate_slice = jnp.dot(
        token_rows_full, up_left_factor, preferred_element_type=jnp.float32
    )
    coords_gate, coords_up = (
        lax.psum(gate_coordinate_slice.astype(jnp.bfloat16), "col").astype(jnp.float32),
        lax.psum(up_coordinate_slice.astype(jnp.bfloat16), "col").astype(jnp.float32),
    )
    first_own = lax.axis_index("col") * own_count
    local_gate_slice = lax.dynamic_slice_in_dim(coords_gate, first_own, own_count, 0)
    local_up_slice = lax.dynamic_slice_in_dim(coords_up, first_own, own_count, 0)
    gate_total = lax.psum_scatter(
        plain_term(token_rows_full, gate_frozen_weight).astype(jnp.bfloat16),
        "col",
        scatter_dimension=0,
        tiled=True,
    ).astype(jnp.float32)
    up_total = lax.psum_scatter(
        plain_term(token_rows_full, up_frozen_weight).astype(jnp.bfloat16),
        "col",
        scatter_dimension=0,
        tiled=True,
    ).astype(jnp.float32)
    gate_total = gate_total + jnp.dot(
        local_gate_slice, gate_right_factor.astype(jnp.float32), precision=lax.Precision.HIGHEST
    )
    up_total = up_total + jnp.dot(
        local_up_slice, up_right_factor.astype(jnp.float32), precision=lax.Precision.HIGHEST
    )
    hidden_values = (
        jax.nn.silu(gate_total * gate_column_scale[None, :]) * (up_total * up_column_scale[None, :])
    ).astype(jnp.bfloat16)
    hidden_full = lax.all_gather(hidden_values, "col", axis=0, tiled=True)
    mixed = lax.psum_scatter(
        rank_update_term(
            hidden_full, down_frozen_weight, down_left_factor, down_right_factor
        ).astype(jnp.bfloat16),
        "row",
        scatter_dimension=0,
        tiled=True,
    ).astype(jnp.float32)
    return (mixed * down_column_scale[None, :]).astype(jnp.bfloat16)


def solution(mesh):
    placed = (
        P("row", "col"),
        P("col", "row"),
        P("col", None),
        P(None, "row"),
        P("row"),
        P("col", "row"),
        P("col", None),
        P(None, "row"),
        P("row"),
        P("row", "col"),
        P("row", None),
        P(None, "col"),
        P("col"),
    )
    return jax.shard_map(
        shards, mesh=mesh, in_specs=placed, out_specs=P("row", "col"), check_vma=False
    )
```

profile of v0, /device:TPU:0, one launch (start us, length us, event | category | flops | bytes accessed | tf_op | source)
XLA Modules:
  0.0 501.4 jit_solution(14623297997536704496)
XLA Ops:
  6.5 0.0 copy-start
  6.5 0.0 all-gather.3.cloned.1.call-start
  6.5 0.7 all-gather.3.cloned.1.call-update
  7.3 0.0 all-reduce.4.cloned.1.call-start
  7.3 50.0 %all-gather.3.cloned.1.call-done = bf16[1024,1024]{1,0:T(8,128)(2,1)} async-done(((bf16[256,1024]{1,0:T(8,128)(2,1)}), bf16[1024,1024]{1,0:T(8,128)(2,1)}) %all-gather.3.cloned.1.call-update) | async-done | bytes 2097168 | tf_op jit(solution)/shard_map/all_gather | solution.py:39
  57.3 0.0 copy-start.1
  57.3 3.1 convolution_convert_fusion.2
  60.4 3.0 convolution_convert_fusion.3
  63.4 0.0 all-reduce.4.cloned.1.call-update
  63.5 0.0 reduce-scatter.4.cloned.1.call-start
  63.5 0.0 copy-done.1
  63.5 23.0 %convolution_convert_fusion.1 = bf16[1024,7168]{1,0:T(8,128)(2,1)} fusion(bf16[1024,1024]{1,0:T(8,128)(2,1)S(1)} %copy-done.1, bf16[1024,7168]{1,0:T(8,128)(2,1)} %param.14), kind=kOutput, calls=%fused_computation.4 | convolution fusion | flops 15039725568 | bytes 31457280 | tf_op jit(solution)/shard_map/dot_general | solution.py:15
  86.5 0.0 reduce-scatter.4.cloned.1.call-update
  86.5 0.0 reduce-scatter.6.cloned.1.call-start
  86.6 23.0 %convolution_convert_fusion = bf16[1024,7168]{1,0:T(8,128)(2,1)} fusion(bf16[1024,1024]{1,0:T(8,128)(2,1)S(1)} %copy-done.1, bf16[1024,7168]{1,0:T(8,128)(2,1)} %param.18), kind=kOutput, calls=%fused_computation.3 | convolution fusion | flops 15039725568 | bytes 31457280 | tf_op jit(solution)/shard_map/dot_general | solution.py:15
  109.6 0.0 copy-start.2
  109.6 0.0 copy-start.9
  109.6 0.0 reduce-scatter.6.cloned.1.call-update
  109.6 0.2 all-gather.5.cloned.1.call-start
  109.9 0.6 copy-done.2
  110.5 0.4 copy-done.9
  110.9 0.0 copy-start.3
  110.9 7.5 %multiply_reduce_fusion.1 = f32[7168]{0:T(1024)S(1)} fusion(bf16[1024,7168]{1,0:T(8,128)(2,1)} %param.18, bf16[1024,64]{0,1:T(8,128)(2,1)S(1)} %copy-done.2, bf16[64,7168]{1,0:T(8,128)(2,1)S(1)} %copy-done.9), kind=kOutput, calls=%fused_computation.1 | convolution fusion | flops 968877056 | bytes 15757312 | tf_op jit(solution)/shard_map/dot_general | solution.py:10
  118.4 0.0 copy-done
  118.4 0.0 copy-done.3
  118.4 0.0 copy-start.5
  118.4 0.0 copy-start.6
  118.4 7.5 %multiply_reduce_fusion.2 = f32[7168]{0:T(1024)S(1)} fusion(bf16[1024,7168]{1,0:T(8,128)(2,1)} %param.14, bf16[1024,64]{0,1:T(8,128)(2,1)S(1)} %copy-done.3, bf16[64,7168]{1,0:T(8,128)(2,1)S(1)} %copy-done), kind=kOutput, calls=%fused_computation.2 | convolution fusion | flops 968877056 | bytes 15757312 | tf_op jit(solution)/shard_map/dot_general | solution.py:10
  125.9 24.2 %all-reduce = (f32[7168]{0:T(1024)S(1)}, f32[7168]{0:T(1024)S(1)}) all-reduce(f32[7168]{0:T(1024)S(1)} %multiply_reduce_fusion.2, f32[7168]{0:T(1024)S(1)} %multiply_reduce_fusion.1), channel_id=1, replica_groups=mesh['row'=4,'col'=8] {'col'}, use_global_device_ids=true, to_apply=%region_3.0 | all-reduce | flops 14336 | bytes 114688 | tf_op jit(solution)/shard_map/psum | solution.py:40
  150.1 0.0 copy-done.5
  150.1 0.0 copy-done.6
  150.2 0.0 all-reduce.4.cloned.1.call-done
  150.2 74.6 %reduce-scatter.4.cloned.1.call-done = bf16[128,7168]{1,0:T(8,128)(2,1)} async-done(((bf16[1024,7168]{1,0:T(8,128)(2,1)}), bf16[128,7168]{1,0:T(8,128)(2,1)}) %reduce-scatter.4.cloned.1.call-update) | async-done | bytes 1835024 | tf_op jit(solution)/shard_map/reduce_scatter | solution.py:67
  224.8 3.9 fusion.2
  228.7 104.1 %reduce-scatter.6.cloned.1.call-done = bf16[128,7168]{1,0:T(8,128)(2,1)} async-done(((bf16[1024,7168]{1,0:T(8,128)(2,1)}), bf16[128,7168]{1,0:T(8,128)(2,1)}) %reduce-scatter.6.cloned.1.call-update) | async-done | bytes 1835024 | tf_op jit(solution)/shard_map/reduce_scatter | solution.py:73
  332.8 0.0 copy-start.10
  332.8 5.4 %fusion.3 = bf16[128,7168]{1,0:T(8,128)(2,1)} fusion(bf16[64,7168]{1,0:T(8,128)(2,1)S(1)} %copy-done.9, bf16[128,7168]{1,0:T(8,128)(2,1)} %reduce-scatter.6.cloned.1.call-done, f32[128,7168]{1,0:T(8,128)} %fusion.2, f32[7168]{0:T(1024)S(1)} %get-tuple-element.9, bf16[1024,64]{1,0:T(8,128)(2,1)} %get-tuple-element.8, s32[]{:T(128)S(6)} %select_n.4), kind=kOutput, calls=%fused_computation.10 | convolution fusion | flops 125698048 | bytes 8318980 | tf_op jit(solution)/shard_map/dot_general | solution.py:82
  338.1 0.0 all-gather.5.cloned.1.call-update
  338.2 0.0 copy-start.4
  338.2 0.3 reduce-scatter.8.cloned.1.call-start
  338.4 80.7 %all-gather.5.cloned.1.call-done = bf16[1024,7168]{1,0:T(8,128)(2,1)} async-done(((bf16[128,7168]{1,0:T(8,128)(2,1)}), bf16[1024,7168]{1,0:T(8,128)(2,1)}) %all-gather.5.cloned.1.call-update) | async-done | bytes 14680080 | tf_op jit(solution)/shard_map/all_gather | solution.py:88
  419.2 0.0 copy-done.10
  419.2 0.0 copy-start.8
  419.2 8.8 %fusion.8 = f32[1024,64]{1,0:T(8,128)S(1)} fusion(bf16[1024,7168]{1,0:T(8,128)(2,1)} %all-gather.5.cloned.1.call-done, bf16[7168,64]{0,1:T(8,128)(2,1)S(1)} %copy-done.10), kind=kOutput, calls=%fused_computation.22 | convolution fusion | flops 939524096 | bytes 15859712 | tf_op jit(solution)/shard_map/dot_general | solution.py:20
  428.0 0.0 copy-done.4
  428.0 1.8 fusion.9
  429.7 0.0 copy-done.8
  429.8 18.8 %add_convert_fusion = bf16[1024,1024]{1,0:T(8,128)(2,1)} fusion(f32[1024,1024]{1,0:T(8,128)S(1)} %fusion.9, bf16[1024,7168]{1,0:T(8,128)(2,1)S(1)} %copy-done.8, bf16[7168,1024]{1,0:T(8,128)(2,1)} %param.22), kind=kOutput, calls=%fused_computation.11 | convolution fusion | flops 15034482688 | bytes 35651584 | tf_op jit(solution)/shard_map/dot_general | solution.py:19
  448.5 0.0 reduce-scatter.8.cloned.1.call-update
  448.5 0.0 copy-start.7
  448.5 7.4 %multiply_reduce_fusion = f32[1024]{0:T(1024)S(1)} fusion(bf16[7168,1024]{1,0:T(8,128)(2,1)} %param.22, bf16[7168,64]{0,1:T(8,128)(2,1)S(1)} %copy-done.10, bf16[64,1024]{1,0:T(8,128)(2,1)S(1)} %copy-done.4), kind=kOutput, calls=%fused_computation | convolution fusion | flops 968883200 | bytes 15732736 | tf_op jit(solution)/shard_map/dot_general | solution.py:10
  456.0 12.3 %psum.39 = f32[1024]{0:T(1024)S(1)} all-reduce(f32[1024]{0:T(1024)S(1)} %multiply_reduce_fusion), channel_id=1, replica_groups=mesh['row'=4,'col'=8] {'row'}, use_global_device_ids=true, to_apply=%region_10.11 | all-reduce | flops 1024 | bytes 8192 | tf_op jit(solution)/shard_map/psum | solution.py:47
  468.2 0.0 copy-done.7
  468.2 24.3 %reduce-scatter.8.cloned.1.call-done = bf16[256,1024]{1,0:T(8,128)(2,1)} async-done(((bf16[1024,1024]{1,0:T(8,128)(2,1)}), bf16[256,1024]{1,0:T(8,128)(2,1)}) %reduce-scatter.8.cloned.1.call-update) | async-done | bytes 524304 | tf_op jit(solution)/shard_map/reduce_scatter | solution.py:89
  492.6 1.9 multiply_convert_fusion
  (2 shorter events, 0.0 us)
Async XLA Ops:
  6.5 111.9 %copy-start = (bf16[64,7168]{1,0:T(8,128)(2,1)S(1)}, bf16[64,7168]{1,0:T(8,128)(2,1)}, u32[]{:S(2)}) copy-start(bf16[64,7168]{1,0:T(8,128)(2,1)} %param.16) | copy-start | bytes 2752516
  6.5 50.8 %all-gather.3.cloned.1.call-start = ((), (), s32[]{:S(2)}) async-start(), calls=%async_computation.3 | async-start | bytes 2621440 | tf_op jit(solution)/shard_map/all_gather | solution.py:39
  7.3 142.9 %all-reduce.4.cloned.1.call-start = ((), (), s32[]{:S(2)}) async-start(), calls=%async_computation.8 | async-start | bytes 1048576 | tf_op jit(solution)/shard_map/psum | solution.py:61
  57.3 6.2 %copy-start.1 = (bf16[1024,1024]{1,0:T(8,128)(2,1)S(1)}, bf16[1024,1024]{1,0:T(8,128)(2,1)}, u32[]{:S(2)}) copy-start(bf16[1024,1024]{1,0:T(8,128)(2,1)} %all-gather.3.cloned.1.call-done) | copy-start | bytes 6291460
  63.5 161.3 %reduce-scatter.4.cloned.1.call-start = ((), (), s32[]{:S(2)}) async-start(), calls=%async_computation.4 | async-start | bytes 16515072 | tf_op jit(solution)/shard_map/reduce_scatter | solution.py:67
  86.5 246.2 %reduce-scatter.6.cloned.1.call-start = ((), (), s32[]{:S(2)}) async-start(), calls=%async_computation.5 | async-start | bytes 16515072 | tf_op jit(solution)/shard_map/reduce_scatter | solution.py:73
  109.6 0.9 copy-start.2
  109.6 1.3 copy-start.9
  109.6 309.6 %all-gather.5.cloned.1.call-start = ((), (), s32[]{:S(2)}) async-start(), calls=%async_computation.6 | async-start | bytes 16515072 | tf_op jit(solution)/shard_map/all_gather | solution.py:88
  110.9 7.5 %copy-start.3 = (bf16[1024,64]{0,1:T(8,128)(2,1)S(1)}, bf16[1024,64]{0,1:T(8,128)(2,1)}, u32[]{:S(2)}) copy-start(bf16[1024,64]{0,1:T(8,128)(2,1)} %param.15) | copy-start | bytes 393220
  118.4 31.7 %copy-start.5 = (f32[7168]{0:T(1024)S(1)}, f32[7168]{0:T(1024)}, u32[]{:S(2)}) copy-start(f32[7168]{0:T(1024)} %param.21) | copy-start | bytes 86020
  118.4 31.7 %copy-start.6 = (f32[7168]{0:T(1024)S(1)}, f32[7168]{0:T(1024)}, u32[]{:S(2)}) copy-start(f32[7168]{0:T(1024)} %param.17) | copy-start | bytes 86020
  332.8 86.4 %copy-start.10 = (bf16[7168,64]{0,1:T(8,128)(2,1)S(1)}, bf16[7168,64]{0,1:T(8,128)(2,1)}, u32[]{:S(2)}) copy-start(bf16[7168,64]{0,1:T(8,128)(2,1)} %param.23) | copy-start | bytes 2752516
  338.2 89.8 %copy-start.4 = (bf16[64,1024]{1,0:T(8,128)(2,1)S(1)}, bf16[64,1024]{1,0:T(8,128)(2,1)}, u32[]{:S(2)}) copy-start(bf16[64,1024]{1,0:T(8,128)(2,1)} %param.24) | copy-start | bytes 393220
  338.2 154.4 %reduce-scatter.8.cloned.1.call-start = ((), (), s32[]{:S(2)}) async-start(), calls=%async_computation.7 | async-start | bytes 2621440 | tf_op jit(solution)/shard_map/reduce_scatter | solution.py:89
  419.2 10.6 %copy-start.8 = (bf16[1024,7168]{1,0:T(8,128)(2,1)S(1)}, bf16[1024,7168]{1,0:T(8,128)(2,1)}, u32[]{:S(2)}) copy-start(bf16[1024,7168]{1,0:T(8,128)(2,1)} %all-gather.5.cloned.1.call-done) | copy-start | bytes 44040196
  448.5 19.7 %copy-start.7 = (f32[1024]{0:T(1024)S(1)}, f32[1024]{0:T(1024)}, u32[]{:S(2)}) copy-start(f32[1024]{0:T(1024)} %param.25) | copy-start | bytes 12292
Sparse Core Ops, SparseCore 0:
  8.9 48.3 all-gather.2
  63.6 53.6 all-reduce.3
  120.8 103.9 reduce-scatter.3
  228.1 104.6 reduce-scatter.5
  338.3 80.8 all-gather.4
  448.7 43.8 reduce-scatter.7
where the time goes:
time: 502 us; the launch traced here: 501 us
  waiting for transfers between devices  335 us (67%)
  matrix products  113 us (23%)
  blocking collectives  36.5 us (7%)
  between operations  13.6 us (3%)
    reduce_scatter x1, waiting for transfers between devices, shards(): lax.psum_scatter(plain_term(token_rows_full, up_frozen_weight).astype(jnp...  104 us
    all_gather x1, waiting for transfers between devices, shards(): hidden_full = lax.all_gather(hidden_values, 'col', axis=0, tiled=True)  80.7 us
    reduce_scatter x1, waiting for transfers between devices, shards(): lax.psum_scatter(plain_term(token_rows_full, gate_frozen_weight).astype(j...  74.6 us
    all_gather x1, waiting for transfers between devices, shards(): token_rows_full = lax.all_gather(tokens, 'row', axis=0, tiled=True)  50 us
    dot_general x2, matrix products, plain_term(): return jnp.dot(inputs, weight, preferred_element_type=jnp.float32)  46 us
    reduce_scatter x1, waiting for transfers between devices, shards(): lax.psum_scatter(rank_update_term(hidden_full, down_frozen_weight, down_l...  24.3 us
    psum x1, blocking collectives, shards(): lax.psum((column_square_totals(gate_frozen_weight, gate_left_factor, gate...  24.2 us
    dot_general x3, matrix products, column_square_totals(): jnp.dot(low_b, low_a, preferred_element_type=jnp.float32)  22.4 us
  transfers between devices with their start and end apart: 6, of which 5 were waited for; matrix products, arithmetic and copies ran while one was open for 14% of the time, Pallas kernels for 0%

commit v1 on v0

v1 whole, which is shorter than its diff:
```python
import jax
import jax.numpy as jnp
from jax import lax
from jax.experimental import pallas as pl
from jax.experimental.pallas import tpu as pltpu
from jax.sharding import PartitionSpec as P


stability_offset = 1e-06
chunk_count = 4
F32, BF16 = jnp.float32, jnp.bfloat16


def column_square_totals(weight, low_b, low_a):
    merged = weight.astype(F32) + jnp.dot(low_b, low_a, preferred_element_type=F32)
    return jnp.sum(merged * merged, axis=0)


def swap(value, axis, size, bit):
    return lax.ppermute(value, axis, [(i, i ^ (1 << bit)) for i in range(size)])


def shift(value, axis, size, by):
    return lax.ppermute(value, axis, [(i, (i + by) % size) for i in range(size)])


def butterfly_sum(value, axis, size):
    for bit in range(size.bit_length() - 1):
        value = value + swap(value, axis, size, bit)
    return value


def gather_rows(block, axis, size):
    found = {0: block}
    right, left = block, block
    for step in range(1, size // 2 + 1):
        if 2 * step == size:
            half = block.shape[0] // 2
            first = shift(right[:half], axis, size, 1)
            second = shift(left[half:], axis, size, -1)
            found[step] = jnp.concatenate([first, second], axis=0)
        else:
            right, left = shift(right, axis, size, 1), shift(left, axis, size, -1)
            found[step], found[size - step] = right, left
    return [found[i] for i in range(size)]


def scatter_sum(blocks, axis, size):
    far = size // 2
    half = blocks[0].shape[0] // 2
    right = blocks[far][:half]
    left = blocks[far][half:]
    for step in range(far, 1, -1):
        right = shift(right, axis, size, 1).astype(F32)
        left = shift(left, axis, size, -1).astype(F32)
        if step == far:
            right = jnp.concatenate([right, jnp.zeros_like(right)], axis=0)
            left = jnp.concatenate([jnp.zeros_like(left), left], axis=0)
        right = (right + blocks[step - 1].astype(F32)).astype(BF16)
        left = (left + blocks[size - step + 1].astype(F32)).astype(BF16)
    right = shift(right, axis, size, 1).astype(F32)
    left = shift(left, axis, size, -1).astype(F32)
    return blocks[0].astype(F32) + right + left


def product_kernel(x_ref, cg_ref, cu_ref, wg_ref, rg_ref, wu_ref, ru_ref, sg, su, kg, ku):
    half = sg.shape[0]
    for w, r, c, s, k in ((wg_ref, rg_ref, cg_ref, sg, kg), (wu_ref, ru_ref, cu_ref, su, ku)):
        total = jnp.dot(x_ref[...], w[...], preferred_element_type=F32)
        total += jnp.dot(c[...], r[...], preferred_element_type=F32)
        k[...] = total[:half].astype(BF16)
        s[...] = total[half:].astype(BF16)


def products(x, cg, cu, wg, rg, wu, ru, chunk, width):
    rows, depth = x.shape
    rank = rg.shape[0]
    tile = next(t for t in (256, 128) if width % t == 0)
    steps = width // tile
    first = chunk * steps
    whole = lambda a: pl.BlockSpec(a.shape, lambda j: (0, 0))
    col = lambda height: pl.BlockSpec((height, tile), lambda j: (0, first + j))
    out = pl.BlockSpec((rows // 2, tile), lambda j: (0, j))
    return pl.pallas_call(
        product_kernel,
        grid=(steps,),
        in_specs=[whole(x), whole(cg), whole(cu), col(depth), col(rank), col(depth), col(rank)],
        out_specs=[out] * 4,
        out_shape=[jax.ShapeDtypeStruct((rows // 2, width), BF16)] * 4,
        cost_estimate=pl.CostEstimate(
            flops=4 * rows * (depth + 4 * rank) * width,
            bytes_accessed=4 * (depth + 2 * rows) * width,
            transcendentals=0,
        ),
        compiler_params=pltpu.CompilerParams(vmem_limit_bytes=48 * 1024 * 1024),
    )(x, cg, cu, wg, rg, wu, ru)


def merge_kernel(w_ref, l_ref, r_ref, merged_ref, squares_ref):
    merged = w_ref[...].astype(F32)
    merged += jnp.dot(l_ref[...], r_ref[...], preferred_element_type=F32)
    merged_ref[...] = merged.astype(BF16)

    @pl.when(pl.program_id(0) == 0)
    def _():
        squares_ref[...] = jnp.zeros_like(squares_ref)

    squares_ref[...] += jnp.sum(merged * merged, axis=0, keepdims=True)


def merge(weight, left, right):
    rows, cols = weight.shape
    rank = left.shape[1]
    tile = next(t for t in (512, 256, 128) if rows % t == 0)
    return pl.pallas_call(
        merge_kernel,
        grid=(rows // tile,),
        in_specs=[
            pl.BlockSpec((tile, cols), lambda i: (i, 0)),
            pl.BlockSpec((tile, rank), lambda i: (i, 0)),
            pl.BlockSpec((rank, cols), lambda i: (0, 0)),
        ],
        out_specs=[
            pl.BlockSpec((tile, cols), lambda i: (i, 0)),
            pl.BlockSpec((1, cols), lambda i: (0, 0)),
        ],
        out_shape=[
            jax.ShapeDtypeStruct((rows, cols), BF16),
            jax.ShapeDtypeStruct((1, cols), F32),
        ],
        cost_estimate=pl.CostEstimate(
            flops=8 * rank * rows * cols,
            bytes_accessed=4 * rows * cols,
            transcendentals=0,
        ),
        compiler_params=pltpu.CompilerParams(vmem_limit_bytes=32 * 1024 * 1024),
    )(weight, left, right)


def add(a, b):
    return (a.astype(F32) + b.astype(F32)).astype(BF16)


def shards(
    n_row,
    n_col,
    tokens,
    gate_frozen_weight,
    gate_left_factor,
    gate_right_factor,
    gate_column_magnitude,
    up_frozen_weight,
    up_left_factor,
    up_right_factor,
    up_column_magnitude,
    down_frozen_weight,
    down_left_factor,
    down_right_factor,
    down_column_magnitude,
):
    me_row, me_col = lax.axis_index("row"), lax.axis_index("col")
    bits = n_col.bit_length() - 1
    chains = [list(range(1, bits)), list(range(bits - 1, 0, -1))]

    by_distance = jnp.stack(gather_rows(tokens, "row", n_row))
    own_rows = tokens.shape[0]
    total_rows = own_rows * n_row
    unit = total_rows // n_col // 2

    gate_sq = column_square_totals(gate_frozen_weight, gate_left_factor, gate_right_factor)
    up_sq = column_square_totals(up_frozen_weight, up_left_factor, up_right_factor)
    squares = butterfly_sum(jnp.stack([gate_sq, up_sq]), "col", n_col)
    gate_scale = gate_column_magnitude / jnp.sqrt(squares[0] + stability_offset)
    up_scale = up_column_magnitude / jnp.sqrt(squares[1] + stability_offset)
    down_merged, down_sq = merge(down_frozen_weight, down_left_factor, down_right_factor)
    down_sq = butterfly_sum(down_sq, "row", n_row)
    down_scale = down_column_magnitude / jnp.sqrt(down_sq[0] + stability_offset)

    order = []
    for low in (0, 1):
        for which, chain in enumerate(chains):
            for index in range(1 << (bits - 1)):
                position = low
                for place, bit in enumerate(chain):
                    if index >> (len(chain) - 1 - place) & 1:
                        position |= 1 << bit
                order.append((position, which))

    def start_of(position, which):
        return ((position ^ me_col) * 2 + which) * unit

    pieces = []
    for position, which in order:
        start = start_of(position, which)
        distance = lax.rem(me_row - start // own_rows + n_row, n_row)
        pieces.append(
            lax.dynamic_slice(
                by_distance,
                (distance, lax.rem(start, own_rows), 0),
                (1, unit, tokens.shape[1]),
            )[0]
        )
    x = jnp.concatenate(pieces, axis=0)
    gate_coords = jnp.dot(x, gate_left_factor, preferred_element_type=F32).astype(BF16)
    up_coords = jnp.dot(x, up_left_factor, preferred_element_type=F32).astype(BF16)

    hidden_units = gate_frozen_weight.shape[1]
    width = hidden_units // chunk_count
    group = unit << (bits - 1)
    low_total = [0.0, 0.0]
    for chunk in range(chunk_count):
        cols = slice(chunk * width, (chunk + 1) * width)
        send_g, send_u, keep_g, keep_u = products(
            x, gate_coords, up_coords,
            gate_frozen_weight, gate_right_factor, up_frozen_weight, up_right_factor,
            chunk, width,
        )
        got_g, got_u = swap(send_g, "col", n_col, 0), swap(send_u, "col", n_col, 0)
        states = []
        for which in (0, 1):
            base = which * group
            states.append(
                [(k[base : base + group], g[base : base + group])
                 for k, g in ((keep_g, got_g), (keep_u, got_u))]
            )
        half = group
        for place in range(bits - 1):
            half //= 2
            for which in (0, 1):
                sums = states[which]
                sends = [add(k[half:], g[half:]) for k, g in sums]
                sends = lax.optimization_barrier(tuple(sends))
                keeps = [add(k[:half], g[:half]) for k, g in sums]
                states[which] = [
                    (k, swap(s, "col", n_col, chains[which][place]))
                    for k, s in zip(keeps, sends)
                ]
        parts = []
        for which in (0, 1):
            gate, up = [k.astype(F32) + g.astype(F32) for k, g in states[which]]
            parts.append(
                (
                    jax.nn.silu(gate * gate_scale[None, cols]) * (up * up_scale[None, cols])
                ).astype(BF16)
            )
        for step in range(bits - 1):
            for which in (0, 1):
                other = swap(parts[which], "col", n_col, chains[which][bits - 2 - step])
                parts[which] = jnp.concatenate([parts[which], other], axis=0)
        near = jnp.concatenate(parts, axis=0)
        far = swap(near, "col", n_col, 0)
        for low, hidden in enumerate((near, far)):
            low_total[low] = low_total[low] + jnp.dot(
                hidden, down_merged[cols], preferred_element_type=F32
            )

    mixed = jnp.concatenate(low_total, axis=0).astype(BF16)

    def place_of(owner, which):
        position = owner ^ me_col
        index = 0
        chain = chains[which]
        for place, bit in enumerate(chain):
            index = index + (((position >> bit) & 1) << (len(chain) - 1 - place))
        return (((position & 1) * 2 + which) * (1 << (bits - 1)) + index) * unit

    blocks = []
    for distance in range(n_row):
        target = lax.rem(me_row + distance, n_row)
        rows = []
        for i in range(own_rows // unit):
            number = target * (own_rows // unit) + i
            owner, which = number // 2, i % 2
            rows.append(
                lax.dynamic_slice_in_dim(mixed, place_of(owner, which), unit, 0)
            )
        blocks.append(jnp.concatenate(rows, axis=0))
    total = scatter_sum(blocks, "row", n_row)
    return (total * down_scale[None, :]).astype(BF16)


def solution(mesh):
    placed = (
        P("row", "col"),
        P("col", "row"),
        P("col", None),
        P(None, "row"),
        P("row"),
        P("col", "row"),
        P("col", None),
        P(None, "row"),
        P("row"),
        P("row", "col"),
        P("row", None),
        P(None, "col"),
        P("col"),
    )

    def body(*arrays):
        return shards(mesh.shape["row"], mesh.shape["col"], *arrays)

    return jax.shard_map(
        body, mesh=mesh, in_specs=placed, out_specs=P("row", "col"), check_vma=False
    )
```

time: 502 us -> 467 us (0.930); the launches traced: 501 us -> 460 us
  waiting for transfers between devices: 335 us -> 249 us
  matrix products: 113 us -> 38.3 us
  Pallas kernels: 0 us -> 69.1 us
  starting transfers between devices: 0.61 us -> 67.6 us
  blocking collectives: 36.5 us -> 0 us
  other arithmetic: 1.97 us -> 24.1 us
  between operations: 13.6 us -> 1.46 us
  local copies, waits for them, and re-layouts: 1.05 us -> 10.2 us
    ppermute x0 -> x73, waiting for transfers between devices: none -> 249 us  [the longest x65 230 us: swap(): return lax.ppermute(value, axis, [(i, i ^ 1 << bit) for i in range(size)])]
    reduce_scatter x3 -> x0, waiting for transfers between devices: 203 us -> none  [the longest x1 104 us: shards(): lax.psum_scatter(plain_term(token_rows_full, up_frozen_weight).astype(jnp...]
    all_gather x2 -> x0, waiting for transfers between devices: 131 us -> none  [the longest x1 80.7 us: shards(): hidden_full = lax.all_gather(hidden_values, 'col', axis=0, tiled=True)]
    dot_general x12, matrix products: 113 us -> 38.3 us  [the longest x8 19.8 us: shards(): jnp.dot(hidden, down_merged[cols], preferred_element_type=F32)]
    pallas_call x0 -> x5, Pallas kernels: none -> 69.1 us  [the longest x4 55 us: products(): pl.pallas_call(product_kernel, grid=(steps,), in_specs=[whole(x), whole(c...]
    ppermute x0 -> x73, starting transfers between devices: none -> 67.6 us  [the longest x65 43.5 us: swap(): return lax.ppermute(value, axis, [(i, i ^ 1 << bit) for i in range(size)])]
    psum x2 -> x0, blocking collectives: 36.5 us -> none  [the longest x1 24.2 us: shards(): lax.psum((column_square_totals(gate_frozen_weight, gate_left_factor, gate...]
    convert_element_type x1 -> x27, other arithmetic: 1.94 us -> 12.8 us  [the longest x24 10.6 us: add(): return (a.astype(F32) + b.astype(F32)).astype(BF16)]
  transfers between devices with their start and end apart: 6 -> 73, of which waited for: 5 -> 41; matrix products, arithmetic and copies ran while one was open for 14% -> 9% of each run, Pallas kernels for 0% -> 12%
where the time goes in v1:
time: 467 us; the launch traced here: 460 us
  waiting for transfers between devices  249 us (53%)
  Pallas kernels  69.1 us (15%)
  starting transfers between devices  67.6 us (14%)
  matrix products  38.3 us (8%)
  other arithmetic  24.1 us (5%)
  local copies, waits for them, and re-layouts  10.2 us (2%)
    ppermute x65, waiting for transfers between devices, swap(): return lax.ppermute(value, axis, [(i, i ^ 1 << bit) for i in range(size)])  230 us
    pallas_call x4, Pallas kernels, products(): pl.pallas_call(product_kernel, grid=(steps,), in_specs=[whole(x), whole(c...  55 us
    ppermute x65, starting transfers between devices, swap(): return lax.ppermute(value, axis, [(i, i ^ 1 << bit) for i in range(size)])  43.5 us
    ppermute x8, starting transfers between devices, shift(): lax.ppermute(value, axis, [(i, (i + by) % size) for i in range(size)])  24.1 us
    dot_general x8, matrix products, shards(): jnp.dot(hidden, down_merged[cols], preferred_element_type=F32)  19.8 us
    ppermute x8, waiting for transfers between devices, shift(): lax.ppermute(value, axis, [(i, (i + by) % size) for i in range(size)])  18.9 us
    dot_general x2, matrix products, column_square_totals(): jnp.dot(low_b, low_a, preferred_element_type=F32)  17.1 us
    pallas_call x1, Pallas kernels, merge(): pl.pallas_call(merge_kernel, grid=(rows // tile,), in_specs=[pl.BlockSpec...  14.2 us
  transfers between devices with their start and end apart: 73, of which 41 were waited for; matrix products, arithmetic and copies ran while one was open for 9% of the time, Pallas kernels for 12%

profile of v1, /device:TPU:0, one launch (start us, length us, event | category | flops | bytes accessed | tf_op | source)
XLA Modules:
  0.0 460.0 jit_solution(5727395290866671424)
XLA Ops:
  0.0 9.7 %multiply_reduce_fusion.1 = f32[7168]{0:T(1024)S(1)} fusion(bf16[1024,7168]{1,0:T(8,128)(2,1)} %wg_ref.7, bf16[1024,64]{0,1:T(8,128)(2,1)} %param.15, bf16[64,7168]{1,0:T(8,128)(2,1)} %rg_ref.7), kind=kOutput, calls=%fused_computation.1 | convolution fusion | flops 968877056 | bytes 15757312 | tf_op jit(solution)/shard_map/dot_general | solution.py:15
  9.7 7.4 %multiply_reduce_fusion = f32[7168]{0:T(1024)S(1)} fusion(bf16[1024,7168]{1,0:T(8,128)(2,1)} %wu_ref.7, bf16[1024,64]{0,1:T(8,128)(2,1)S(1)} %copy-done, bf16[64,7168]{1,0:T(8,128)(2,1)S(1)} %copy-done.4), kind=kOutput, calls=%fused_computation | convolution fusion | flops 968877056 | bytes 15757312 | tf_op jit(solution)/shard_map/dot_general | solution.py:15
  19.4 2.8 collective-permute-start.10
  22.2 3.6 collective-permute-start.2
  25.8 1.9 copy.16.l_ref
  30.8 14.2 %shard_map.128 = (bf16[7168,1024]{1,0:T(8,128)(2,1)S(1)}, f32[1,1024]{1,0:T(1,128)S(1)}) custom-call(bf16[7168,1024]{1,0:T(8,128)(2,1)} %w_ref.1, bf16[7168,64]{1,0:T(8,128)(2,1)S(1)} %copy.16.l_ref, bf16[64,1024]{1,0:T(8,128)(2,1)S(1)} %copy-done.2), custom_call_target="tpu_custom_call" | custom-call | flops 3758096384 | bytes 29360128 | tf_op jit(solution)/shard_map/pallas_call | solution.py:115
  45.0 5.1 %copy-done.3 = bf16[7168,1024]{1,0:T(8,128)(2,1)} copy-done((bf16[7168,1024]{1,0:T(8,128)(2,1)}, bf16[7168,1024]{1,0:T(8,128)(2,1)S(1)}, u32[]{:S(2)}) %copy-start.3) | copy-done | bytes 14680088
  51.0 3.9 collective-permute-start.3
  55.9 12.3 %collective-permute-start.1 = (bf16[128,1024]{1,0:T(8,128)(2,1)S(1)}, bf16[128,1024]{1,0:T(8,128)(2,1)S(1)}, u32[]{:S(2)}, u32[]{:S(2)}) collective-permute-start(bf16[128,1024]{1,0:T(8,128)(2,1)S(1)} %slice.688), channel_id=1, source_target_pairs={{0,8},{8,16},{16,24},{24,0},{1,9},{9,17},{17,25},{25,1},{2,10},{10... | collective-permute-start | bytes 786440 | tf_op jit(solution)/shard_map/ppermute | solution.py:24
  68.3 8.6 %collective-permute-done.1 = bf16[128,1024]{1,0:T(8,128)(2,1)S(1)} collective-permute-done((bf16[128,1024]{1,0:T(8,128)(2,1)S(1)}, bf16[128,1024]{1,0:T(8,128)(2,1)S(1)}, u32[]{:S(2)}, u32[]{:S(2)}) %collective-permute-start.1) | collective-permute-done | bytes 262176 | tf_op jit(solution)/shard_map/ppermute | solution.py:24
  80.8 13.7 %shard_map.131 = (bf16[512,1792]{1,0:T(8,128)(2,1)}, bf16[512,1792]{1,0:T(8,128)(2,1)}, bf16[512,1792]{1,0:T(8,128)(2,1)}, bf16[512,1792]{1,0:T(8,128)(2,1)}) custom-call(bf16[1024,1024]{1,0:T(8,128)(2,1)} %copy-done.6, bf16[1024,64]{1,0:T(8,128)(2,1)S(1)} %convolution_convert_fusion.1.cg_ref, bf16[1024,64]{1,0:T(8,128)(2,1)S(1)} %convolution_convert_fusion.cu_ref, ...), custom_call_target="tpu_custom_call" | custom-call | flops 9395240960 | bytes 22020096 | tf_op jit(solution)/shard_map/pallas_call | solution.py:84
  94.4 13.8 %shard_map.130 = (bf16[512,1792]{1,0:T(8,128)(2,1)S(1)}, bf16[512,1792]{1,0:T(8,128)(2,1)S(1)}, bf16[512,1792]{1,0:T(8,128)(2,1)}, bf16[512,1792]{1,0:T(8,128)(2,1)}) custom-call(bf16[1024,1024]{1,0:T(8,128)(2,1)} %copy-done.6, bf16[1024,64]{1,0:T(8,128)(2,1)S(1)} %convolution_convert_fusion.1.cg_ref, bf16[1024,64]{1,0:T(8,128)(2,1)S(1)} %convolution_convert_fusion.cu_ref, ...), custom_call_target="tpu_custom_call" | custom-call | flops 9395240960 | bytes 22020096 | tf_op jit(solution)/shard_map/pallas_call | solution.py:84
  108.7 13.7 %shard_map.129 = (bf16[512,1792]{1,0:T(8,128)(2,1)S(1)}, bf16[512,1792]{1,0:T(8,128)(2,1)S(1)}, bf16[512,1792]{1,0:T(8,128)(2,1)}, bf16[512,1792]{1,0:T(8,128)(2,1)}) custom-call(bf16[1024,1024]{1,0:T(8,128)(2,1)} %copy-done.6, bf16[1024,64]{1,0:T(8,128)(2,1)S(1)} %convolution_convert_fusion.1.cg_ref, bf16[1024,64]{1,0:T(8,128)(2,1)S(1)} %convolution_convert_fusion.cu_ref, ...), custom_call_target="tpu_custom_call" | custom-call | flops 9395240960 | bytes 22020096 | tf_op jit(solution)/shard_map/pallas_call | solution.py:84
  122.9 13.8 %shard_map.127 = (bf16[512,1792]{1,0:T(8,128)(2,1)S(1)}, bf16[512,1792]{1,0:T(8,128)(2,1)S(1)}, bf16[512,1792]{1,0:T(8,128)(2,1)}, bf16[512,1792]{1,0:T(8,128)(2,1)}) custom-call(bf16[1024,1024]{1,0:T(8,128)(2,1)} %copy-done.6, bf16[1024,64]{1,0:T(8,128)(2,1)S(1)} %convolution_convert_fusion.1.cg_ref, bf16[1024,64]{1,0:T(8,128)(2,1)S(1)} %convolution_convert_fusion.cu_ref, ...), custom_call_target="tpu_custom_call" | custom-call | flops 9395240960 | bytes 22020096 | tf_op jit(solution)/shard_map/pallas_call | solution.py:84
  137.3 2.0 add_convert_fusion.7
  139.4 2.0 add_convert_fusion.4
  141.9 2.0 add_convert_fusion.15
  144.5 2.0 add_convert_fusion.12
  153.1 4.3 collective-permute-done.51
  158.0 9.2 %collective-permute-done.52 = bf16[128,1792]{1,0:T(8,128)(2,1)S(1)} collective-permute-done((bf16[128,1792]{1,0:T(8,128)(2,1)S(1)}, bf16[128,1792]{1,0:T(8,128)(2,1)S(1)}, u32[]{:S(2)}, u32[]{:S(2)}) %collective-permute-start.52) | collective-permute-done | bytes 458784 | tf_op jit(solution)/shard_map/ppermute | solution.py:20
  169.4 2.4 collective-permute-done.58
  172.4 4.6 %collective-permute-done.37 = bf16[128,1792]{1,0:T(8,128)(2,1)S(1)} collective-permute-done((bf16[128,1792]{1,0:T(8,128)(2,1)S(1)}, bf16[128,1792]{1,0:T(8,128)(2,1)S(1)}, u32[]{:S(2)}, u32[]{:S(2)}) %collective-permute-start.37) | collective-permute-done | bytes 458784 | tf_op jit(solution)/shard_map/ppermute | solution.py:20
  177.6 9.2 %collective-permute-done.38 = bf16[128,1792]{1,0:T(8,128)(2,1)S(1)} collective-permute-done((bf16[128,1792]{1,0:T(8,128)(2,1)S(1)}, bf16[128,1792]{1,0:T(8,128)(2,1)S(1)}, u32[]{:S(2)}, u32[]{:S(2)}) %collective-permute-start.38) | collective-permute-done | bytes 458784 | tf_op jit(solution)/shard_map/ppermute | solution.py:20
  189.1 2.4 collective-permute-done.44
  192.1 4.6 %collective-permute-done.23 = bf16[128,1792]{1,0:T(8,128)(2,1)S(1)} collective-permute-done((bf16[128,1792]{1,0:T(8,128)(2,1)S(1)}, bf16[128,1792]{1,0:T(8,128)(2,1)S(1)}, u32[]{:S(2)}, u32[]{:S(2)}) %collective-permute-start.23) | collective-permute-done | bytes 458784 | tf_op jit(solution)/shard_map/ppermute | solution.py:20
  197.3 9.2 %collective-permute-done.24 = bf16[128,1792]{1,0:T(8,128)(2,1)S(1)} collective-permute-done((bf16[128,1792]{1,0:T(8,128)(2,1)S(1)}, bf16[128,1792]{1,0:T(8,128)(2,1)S(1)}, u32[]{:S(2)}, u32[]{:S(2)}) %collective-permute-start.24) | collective-permute-done | bytes 458784 | tf_op jit(solution)/shard_map/ppermute | solution.py:20
  208.8 2.4 collective-permute-done.30
  211.7 4.6 %collective-permute-done.6 = bf16[128,1792]{1,0:T(8,128)(2,1)S(1)} collective-permute-done((bf16[128,1792]{1,0:T(8,128)(2,1)S(1)}, bf16[128,1792]{1,0:T(8,128)(2,1)S(1)}, u32[]{:S(2)}, u32[]{:S(2)}) %collective-permute-start.6) | collective-permute-done | bytes 458784 | tf_op jit(solution)/shard_map/ppermute | solution.py:20
  216.9 8.4 %collective-permute-done.7 = bf16[128,1792]{1,0:T(8,128)(2,1)S(1)} collective-permute-done((bf16[128,1792]{1,0:T(8,128)(2,1)S(1)}, bf16[128,1792]{1,0:T(8,128)(2,1)S(1)}, u32[]{:S(2)}, u32[]{:S(2)}) %collective-permute-start.7) | collective-permute-done | bytes 458784 | tf_op jit(solution)/shard_map/ppermute | solution.py:20
  227.5 3.3 collective-permute-done.16
  231.4 4.3 collective-permute-done.53
  236.2 4.4 collective-permute-done.54
  241.5 4.1 collective-permute-done.39
  246.1 4.4 collective-permute-done.40
  251.3 4.1 collective-permute-done.25
  255.9 4.4 collective-permute-done.26
  261.1 4.1 collective-permute-done.8
  265.8 2.9 collective-permute-done.12
  269.5 5.4 %collective-permute-done.55 = bf16[64,1792]{1,0:T(8,128)(2,1)S(1)} collective-permute-done((bf16[64,1792]{1,0:T(8,128)(2,1)S(1)}, bf16[64,1792]{1,0:T(8,128)(2,1)S(1)}, u32[]{:S(2)}, u32[]{:S(2)}) %collective-permute-start.55) | collective-permute-done | bytes 229408 | tf_op jit(solution)/shard_map/ppermute | solution.py:20
  275.5 6.2 %collective-permute-done.41 = bf16[64,1792]{1,0:T(8,128)(2,1)S(1)} collective-permute-done((bf16[64,1792]{1,0:T(8,128)(2,1)S(1)}, bf16[64,1792]{1,0:T(8,128)(2,1)S(1)}, u32[]{:S(2)}, u32[]{:S(2)}) %collective-permute-start.41) | collective-permute-done | bytes 229408 | tf_op jit(solution)/shard_map/ppermute | solution.py:20
  282.2 7.3 %collective-permute-done.27 = bf16[64,1792]{1,0:T(8,128)(2,1)S(1)} collective-permute-done((bf16[64,1792]{1,0:T(8,128)(2,1)S(1)}, bf16[64,1792]{1,0:T(8,128)(2,1)S(1)}, u32[]{:S(2)}, u32[]{:S(2)}) %collective-permute-start.27) | collective-permute-done | bytes 229408 | tf_op jit(solution)/shard_map/ppermute | solution.py:20
  290.1 5.4 %collective-permute-done.13 = bf16[64,1792]{1,0:T(8,128)(2,1)S(1)} collective-permute-done((bf16[64,1792]{1,0:T(8,128)(2,1)S(1)}, bf16[64,1792]{1,0:T(8,128)(2,1)S(1)}, u32[]{:S(2)}, u32[]{:S(2)}) %collective-permute-start.13) | collective-permute-done | bytes 229408 | tf_op jit(solution)/shard_map/ppermute | solution.py:20
  296.2 12.0 %collective-permute-done.56 = bf16[128,1792]{1,0:T(8,128)(2,1)S(1)} collective-permute-done((bf16[128,1792]{1,0:T(8,128)(2,1)S(1)}, bf16[128,1792]{1,0:T(8,128)(2,1)S(1)}, u32[]{:S(2)}, u32[]{:S(2)}) %collective-permute-start.56) | collective-permute-done | bytes 458784 | tf_op jit(solution)/shard_map/ppermute | solution.py:20
  311.2 17.5 %collective-permute-done.42 = bf16[128,1792]{1,0:T(8,128)(2,1)S(1)} collective-permute-done((bf16[128,1792]{1,0:T(8,128)(2,1)S(1)}, bf16[128,1792]{1,0:T(8,128)(2,1)S(1)}, u32[]{:S(2)}, u32[]{:S(2)}) %collective-permute-start.42) | collective-permute-done | bytes 458784 | tf_op jit(solution)/shard_map/ppermute | solution.py:20
  331.7 17.5 %collective-permute-done.28 = bf16[128,1792]{1,0:T(8,128)(2,1)S(1)} collective-permute-done((bf16[128,1792]{1,0:T(8,128)(2,1)S(1)}, bf16[128,1792]{1,0:T(8,128)(2,1)S(1)}, u32[]{:S(2)}, u32[]{:S(2)}) %collective-permute-start.28) | collective-permute-done | bytes 458784 | tf_op jit(solution)/shard_map/ppermute | solution.py:20
  352.2 10.4 %collective-permute-done.14 = bf16[128,1792]{1,0:T(8,128)(2,1)S(1)} collective-permute-done((bf16[128,1792]{1,0:T(8,128)(2,1)S(1)}, bf16[128,1792]{1,0:T(8,128)(2,1)S(1)}, u32[]{:S(2)}, u32[]{:S(2)}) %collective-permute-start.14) | collective-permute-done | bytes 458784 | tf_op jit(solution)/shard_map/ppermute | solution.py:20
  368.6 1.8 collective-permute-done.33
  373.6 4.3 collective-permute-done.62
  378.1 4.6 %collective-permute-done.48 = bf16[128,1792]{1,0:T(8,128)(2,1)S(1)} collective-permute-done((bf16[128,1792]{1,0:T(8,128)(2,1)S(1)}, bf16[128,1792]{1,0:T(8,128)(2,1)S(1)}, u32[]{:S(2)}, u32[]{:S(2)}) %collective-permute-start.48) | collective-permute-done | bytes 458784 | tf_op jit(solution)/shard_map/ppermute | solution.py:20
  382.9 4.8 %collective-permute-done.34 = bf16[128,1792]{1,0:T(8,128)(2,1)S(1)} collective-permute-done((bf16[128,1792]{1,0:T(8,128)(2,1)S(1)}, bf16[128,1792]{1,0:T(8,128)(2,1)S(1)}, u32[]{:S(2)}, u32[]{:S(2)}) %collective-permute-start.34) | collective-permute-done | bytes 458784 | tf_op jit(solution)/shard_map/ppermute | solution.py:20
  387.8 4.8 %collective-permute-done.20 = bf16[128,1792]{1,0:T(8,128)(2,1)S(1)} collective-permute-done((bf16[128,1792]{1,0:T(8,128)(2,1)S(1)}, bf16[128,1792]{1,0:T(8,128)(2,1)S(1)}, u32[]{:S(2)}, u32[]{:S(2)}) %collective-permute-start.20) | collective-permute-done | bytes 458784 | tf_op jit(solution)/shard_map/ppermute | solution.py:20
  392.8 2.1 fusion.6
  394.8 2.1 fusion.10
  396.9 3.4 fusion.14
  400.3 3.9 add_convert_fusion.1
  404.2 2.1 fusion.12
  406.2 2.1 fusion.8
  408.3 2.1 fusion.4
  410.4 2.2 add_convert_fusion
  416.2 2.0 collective-permute-start.67
  418.7 10.3 %collective-permute-done.69 = bf16[128,1024]{1,0:T(8,128)(2,1)S(1)} collective-permute-done((bf16[128,1024]{1,0:T(8,128)(2,1)}, bf16[128,1024]{1,0:T(8,128)(2,1)S(1)}, u32[]{:S(2)}, u32[]{:S(2)}) %collective-permute-start.69) | collective-permute-done | bytes 262176 | tf_op jit(solution)/shard_map/ppermute | solution.py:24
  430.3 2.1 collective-permute-start.68
  432.4 21.5 %collective-permute-done.71 = f32[1,1024]{1,0:T(1,128)S(1)} collective-permute-done((f32[1,1024]{1,0:T(1,128)S(1)}, f32[1,1024]{1,0:T(1,128)S(1)}, u32[]{:S(2)}, u32[]{:S(2)}) %collective-permute-start.71) | collective-permute-done | bytes 4128 | tf_op jit(solution)/shard_map/ppermute | solution.py:20
  454.1 4.3 collective-permute-done.72
  (248 shorter events, 66.7 us)
Async XLA Ops:
  22.2 28.8 %collective-permute-start.2 = (bf16[256,1024]{1,0:T(8,128)(2,1)}, bf16[256,1024]{1,0:T(8,128)(2,1)S(1)}, u32[]{:S(2)}, u32[]{:S(2)}) collective-permute-start(bf16[256,1024]{1,0:T(8,128)(2,1)} %param.13), channel_id=1, source_target_pairs={{0,24},{8,0},{16,8},{24,16},{1,25},{9,1},{17,9},{25,17},{2,26},{10... | collective-permute-start | bytes 1572872 | tf_op jit(solution)/shard_map/ppermute | solution.py:24
  25.8 29.1 %collective-permute-start = (bf16[256,1024]{1,0:T(8,128)(2,1)}, bf16[256,1024]{1,0:T(8,128)(2,1)}, u32[]{:S(2)}, u32[]{:S(2)}) collective-permute-start(bf16[256,1024]{1,0:T(8,128)(2,1)} %param.13), channel_id=1, source_target_pairs={{0,8},{8,16},{16,24},{24,0},{1,9},{9,17},{17,25},{25,1},{2,10},{10... | collective-permute-start | bytes 1572872 | tf_op jit(solution)/shard_map/ppermute | solution.py:24
  29.3 20.8 %collective-permute-start.11 = (f32[2,7168]{1,0:T(2,128)}, f32[2,7168]{1,0:T(2,128)}, u32[]{:S(2)}, u32[]{:S(2)}) collective-permute-start(f32[2,7168]{1,0:T(2,128)} %fusion.53), channel_id=1, source_target_pairs={{0,4},{1,5},{2,6},{3,7},{4,0},{5,1},{6,2},{7,3},{8,12},{9,13},{10,... | collective-permute-start | bytes 172040 | tf_op jit(solution)/shard_map/ppermute | solution.py:20
  51.0 17.3 %collective-permute-start.3 = (bf16[128,1024]{1,0:T(8,128)(2,1)S(1)}, bf16[128,1024]{1,0:T(8,128)(2,1)S(1)}, u32[]{:S(2)}, u32[]{:S(2)}) collective-permute-start(bf16[128,1024]{1,0:T(8,128)(2,1)S(1)} %slice.689), channel_id=1, source_target_pairs={{0,24},{8,0},{16,8},{24,16},{1,25},{9,1},{17,9},{25,17},{2,26},{10... | collective-permute-start | bytes 786440 | tf_op jit(solution)/shard_map/ppermute | solution.py:24
  55.9 21.0 %collective-permute-start.1 = (bf16[128,1024]{1,0:T(8,128)(2,1)S(1)}, bf16[128,1024]{1,0:T(8,128)(2,1)S(1)}, u32[]{:S(2)}, u32[]{:S(2)}) collective-permute-start(bf16[128,1024]{1,0:T(8,128)(2,1)S(1)} %slice.688), channel_id=1, source_target_pairs={{0,8},{8,16},{16,24},{24,0},{1,9},{9,17},{17,25},{25,1},{2,10},{10... | collective-permute-start | bytes 786440 | tf_op jit(solution)/shard_map/ppermute | solution.py:24
  94.4 42.4 %collective-permute-start.49 = (bf16[512,1792]{1,0:T(8,128)(2,1)}, bf16[512,1792]{1,0:T(8,128)(2,1)}, u32[]{:S(2)}, u32[]{:S(2)}) collective-permute-start(bf16[512,1792]{1,0:T(8,128)(2,1)} %get-tuple-element.93), channel_id=1, source_target_pairs={{0,1},{1,0},{2,3},{3,2},{4,5},{5,4},{6,7},{7,6},{8,9},{9,8},{10,11... | collective-permute-start | bytes 5505032 | tf_op jit(solution)/shard_map/ppermute | solution.py:20
  108.2 31.0 %collective-permute-start.50 = (bf16[512,1792]{1,0:T(8,128)(2,1)}, bf16[512,1792]{1,0:T(8,128)(2,1)}, u32[]{:S(2)}, u32[]{:S(2)}) collective-permute-start(bf16[512,1792]{1,0:T(8,128)(2,1)} %get-tuple-element.95), channel_id=1, source_target_pairs={{0,1},{1,0},{2,3},{3,2},{4,5},{5,4},{6,7},{7,6},{8,9},{9,8},{10,11... | collective-permute-start | bytes 5505032 | tf_op jit(solution)/shard_map/ppermute | solution.py:20
  122.4 19.0 %collective-permute-start.35 = (bf16[512,1792]{1,0:T(8,128)(2,1)S(1)}, bf16[512,1792]{1,0:T(8,128)(2,1)}, u32[]{:S(2)}, u32[]{:S(2)}) collective-permute-start(bf16[512,1792]{1,0:T(8,128)(2,1)S(1)} %get-tuple-element.81), channel_id=1, source_target_pairs={{0,1},{1,0},{2,3},{3,2},{4,5},{5,4},{6,7},{7,6},{8,9},{9,8},{10,11... | collective-permute-start | bytes 5505032 | tf_op jit(solution)/shard_map/ppermute | solution.py:20
  122.5 21.5 %collective-permute-start.36 = (bf16[512,1792]{1,0:T(8,128)(2,1)S(1)}, bf16[512,1792]{1,0:T(8,128)(2,1)}, u32[]{:S(2)}, u32[]{:S(2)}) collective-permute-start(bf16[512,1792]{1,0:T(8,128)(2,1)S(1)} %get-tuple-element.83), channel_id=1, source_target_pairs={{0,1},{1,0},{2,3},{3,2},{4,5},{5,4},{6,7},{7,6},{8,9},{9,8},{10,11... | collective-permute-start | bytes 5505032 | tf_op jit(solution)/shard_map/ppermute | solution.py:20
  136.7 9.8 %collective-permute-start.21 = (bf16[512,1792]{1,0:T(8,128)(2,1)S(1)}, bf16[512,1792]{1,0:T(8,128)(2,1)S(1)}, u32[]{:S(2)}, u32[]{:S(2)}) collective-permute-start(bf16[512,1792]{1,0:T(8,128)(2,1)S(1)} %get-tuple-element.69), channel_id=1, source_target_pairs={{0,1},{1,0},{2,3},{3,2},{4,5},{5,4},{6,7},{7,6},{8,9},{9,8},{10,11... | collective-permute-start | bytes 5505032 | tf_op jit(solution)/shard_map/ppermute | solution.py:20
  136.8 11.7 %collective-permute-start.22 = (bf16[512,1792]{1,0:T(8,128)(2,1)S(1)}, bf16[512,1792]{1,0:T(8,128)(2,1)S(1)}, u32[]{:S(2)}, u32[]{:S(2)}) collective-permute-start(bf16[512,1792]{1,0:T(8,128)(2,1)S(1)} %get-tuple-element.71), channel_id=1, source_target_pairs={{0,1},{1,0},{2,3},{3,2},{4,5},{5,4},{6,7},{7,6},{8,9},{9,8},{10,11... | collective-permute-start | bytes 5505032 | tf_op jit(solution)/shard_map/ppermute | solution.py:20
  139.3 10.8 %collective-permute-start.4 = (bf16[512,1792]{1,0:T(8,128)(2,1)S(1)}, bf16[512,1792]{1,0:T(8,128)(2,1)S(1)}, u32[]{:S(2)}, u32[]{:S(2)}) collective-permute-start(bf16[512,1792]{1,0:T(8,128)(2,1)S(1)} %get-tuple-element.56), channel_id=1, source_target_pairs={{0,1},{1,0},{2,3},{3,2},{4,5},{5,4},{6,7},{7,6},{8,9},{9,8},{10,11... | collective-permute-start | bytes 5505032 | tf_op jit(solution)/shard_map/ppermute | solution.py:20
  141.4 10.2 %collective-permute-start.5 = (bf16[512,1792]{1,0:T(8,128)(2,1)S(1)}, bf16[512,1792]{1,0:T(8,128)(2,1)S(1)}, u32[]{:S(2)}, u32[]{:S(2)}) collective-permute-start(bf16[512,1792]{1,0:T(8,128)(2,1)S(1)} %get-tuple-element.58), channel_id=1, source_target_pairs={{0,1},{1,0},{2,3},{3,2},{4,5},{5,4},{6,7},{7,6},{8,9},{9,8},{10,11... | collective-permute-start | bytes 5505032 | tf_op jit(solution)/shard_map/ppermute | solution.py:20
  143.9 13.5 %collective-permute-start.51 = (bf16[128,1792]{1,0:T(8,128)(2,1)S(1)}, bf16[128,1792]{1,0:T(8,128)(2,1)S(1)}, u32[]{:S(2)}, u32[]{:S(2)}) collective-permute-start(bf16[128,1792]{1,0:T(8,128)(2,1)S(1)} %get-tuple-element.96), channel_id=1, source_target_pairs={{0,2},{1,3},{2,0},{3,1},{4,6},{5,7},{6,4},{7,5},{8,10},{9,11},{10,... | collective-permute-start | bytes 1376264 | tf_op jit(solution)/shard_map/ppermute | solution.py:20
  146.5 20.7 %collective-permute-start.52 = (bf16[128,1792]{1,0:T(8,128)(2,1)S(1)}, bf16[128,1792]{1,0:T(8,128)(2,1)S(1)}, u32[]{:S(2)}, u32[]{:S(2)}) collective-permute-start(bf16[128,1792]{1,0:T(8,128)(2,1)S(1)} %get-tuple-element.97), channel_id=1, source_target_pairs={{0,2},{1,3},{2,0},{3,1},{4,6},{5,7},{6,4},{7,5},{8,10},{9,11},{10,... | collective-permute-start | bytes 1376264 | tf_op jit(solution)/shard_map/ppermute | solution.py:20
  148.5 19.2 %collective-permute-start.57 = (bf16[128,1792]{1,0:T(8,128)(2,1)S(1)}, bf16[128,1792]{1,0:T(8,128)(2,1)S(1)}, u32[]{:S(2)}, u32[]{:S(2)}) collective-permute-start(bf16[128,1792]{1,0:T(8,128)(2,1)S(1)} %get-tuple-element.100), channel_id=1, source_target_pairs={{0,4},{1,5},{2,6},{3,7},{4,0},{5,1},{6,2},{7,3},{8,12},{9,13},{10,... | collective-permute-start | bytes 1376264 | tf_op jit(solution)/shard_map/ppermute | solution.py:20
  150.0 21.8 %collective-permute-start.58 = (bf16[128,1792]{1,0:T(8,128)(2,1)S(1)}, bf16[128,1792]{1,0:T(8,128)(2,1)S(1)}, u32[]{:S(2)}, u32[]{:S(2)}) collective-permute-start(bf16[128,1792]{1,0:T(8,128)(2,1)S(1)} %get-tuple-element.101), channel_id=1, source_target_pairs={{0,4},{1,5},{2,6},{3,7},{4,0},{5,1},{6,2},{7,3},{8,12},{9,13},{10,... | collective-permute-start | bytes 1376264 | tf_op jit(solution)/shard_map/ppermute | solution.py:20
  151.6 25.4 %collective-permute-start.37 = (bf16[128,1792]{1,0:T(8,128)(2,1)S(1)}, bf16[128,1792]{1,0:T(8,128)(2,1)S(1)}, u32[]{:S(2)}, u32[]{:S(2)}) collective-permute-start(bf16[128,1792]{1,0:T(8,128)(2,1)S(1)} %get-tuple-element.84), channel_id=1, source_target_pairs={{0,2},{1,3},{2,0},{3,1},{4,6},{5,7},{6,4},{7,5},{8,10},{9,11},{10,... | collective-permute-start | bytes 1376264 | tf_op jit(solution)/shard_map/ppermute | solution.py:20
  157.4 29.5 %collective-permute-start.38 = (bf16[128,1792]{1,0:T(8,128)(2,1)S(1)}, bf16[128,1792]{1,0:T(8,128)(2,1)S(1)}, u32[]{:S(2)}, u32[]{:S(2)}) collective-permute-start(bf16[128,1792]{1,0:T(8,128)(2,1)S(1)} %get-tuple-element.85), channel_id=1, source_target_pairs={{0,2},{1,3},{2,0},{3,1},{4,6},{5,7},{6,4},{7,5},{8,10},{9,11},{10,... | collective-permute-start | bytes 1376264 | tf_op jit(solution)/shard_map/ppermute | solution.py:20
  167.2 20.2 %collective-permute-start.43 = (bf16[128,1792]{1,0:T(8,128)(2,1)S(1)}, bf16[128,1792]{1,0:T(8,128)(2,1)S(1)}, u32[]{:S(2)}, u32[]{:S(2)}) collective-permute-start(bf16[128,1792]{1,0:T(8,128)(2,1)S(1)} %get-tuple-element.88), channel_id=1, source_target_pairs={{0,4},{1,5},{2,6},{3,7},{4,0},{5,1},{6,2},{7,3},{8,12},{9,13},{10,... | collective-permute-start | bytes 1376264 | tf_op jit(solution)/shard_map/ppermute | solution.py:20
  167.8 23.7 %collective-permute-start.44 = (bf16[128,1792]{1,0:T(8,128)(2,1)S(1)}, bf16[128,1792]{1,0:T(8,128)(2,1)S(1)}, u32[]{:S(2)}, u32[]{:S(2)}) collective-permute-start(bf16[128,1792]{1,0:T(8,128)(2,1)S(1)} %get-tuple-element.89), channel_id=1, source_target_pairs={{0,4},{1,5},{2,6},{3,7},{4,0},{5,1},{6,2},{7,3},{8,12},{9,13},{10,... | collective-permute-start | bytes 1376264 | tf_op jit(solution)/shard_map/ppermute | solution.py:20
  171.8 24.9 %collective-permute-start.23 = (bf16[128,1792]{1,0:T(8,128)(2,1)S(1)}, bf16[128,1792]{1,0:T(8,128)(2,1)S(1)}, u32[]{:S(2)}, u32[]{:S(2)}) collective-permute-start(bf16[128,1792]{1,0:T(8,128)(2,1)S(1)} %get-tuple-element.72), channel_id=1, source_target_pairs={{0,2},{1,3},{2,0},{3,1},{4,6},{5,7},{6,4},{7,5},{8,10},{9,11},{10,... | collective-permute-start | bytes 1376264 | tf_op jit(solution)/shard_map/ppermute | solution.py:20
  177.0 29.5 %collective-permute-start.24 = (bf16[128,1792]{1,0:T(8,128)(2,1)S(1)}, bf16[128,1792]{1,0:T(8,128)(2,1)S(1)}, u32[]{:S(2)}, u32[]{:S(2)}) collective-permute-start(bf16[128,1792]{1,0:T(8,128)(2,1)S(1)} %get-tuple-element.73), channel_id=1, source_target_pairs={{0,2},{1,3},{2,0},{3,1},{4,6},{5,7},{6,4},{7,5},{8,10},{9,11},{10,... | collective-permute-start | bytes 1376264 | tf_op jit(solution)/shard_map/ppermute | solution.py:20
  186.9 20.2 %collective-permute-start.29 = (bf16[128,1792]{1,0:T(8,128)(2,1)S(1)}, bf16[128,1792]{1,0:T(8,128)(2,1)S(1)}, u32[]{:S(2)}, u32[]{:S(2)}) collective-permute-start(bf16[128,1792]{1,0:T(8,128)(2,1)S(1)} %get-tuple-element.76), channel_id=1, source_target_pairs={{0,4},{1,5},{2,6},{3,7},{4,0},{5,1},{6,2},{7,3},{8,12},{9,13},{10,... | collective-permute-start | bytes 1376264 | tf_op jit(solution)/shard_map/ppermute | solution.py:20
  187.5 23.7 %collective-permute-start.30 = (bf16[128,1792]{1,0:T(8,128)(2,1)S(1)}, bf16[128,1792]{1,0:T(8,128)(2,1)S(1)}, u32[]{:S(2)}, u32[]{:S(2)}) collective-permute-start(bf16[128,1792]{1,0:T(8,128)(2,1)S(1)} %get-tuple-element.77), channel_id=1, source_target_pairs={{0,4},{1,5},{2,6},{3,7},{4,0},{5,1},{6,2},{7,3},{8,12},{9,13},{10,... | collective-permute-start | bytes 1376264 | tf_op jit(solution)/shard_map/ppermute | solution.py:20
  191.5 24.9 %collective-permute-start.6 = (bf16[128,1792]{1,0:T(8,128)(2,1)S(1)}, bf16[128,1792]{1,0:T(8,128)(2,1)S(1)}, u32[]{:S(2)}, u32[]{:S(2)}) collective-permute-start(bf16[128,1792]{1,0:T(8,128)(2,1)S(1)} %get-tuple-element.59), channel_id=1, source_target_pairs={{0,2},{1,3},{2,0},{3,1},{4,6},{5,7},{6,4},{7,5},{8,10},{9,11},{10,... | collective-permute-start | bytes 1376264 | tf_op jit(solution)/shard_map/ppermute | solution.py:20
  196.7 28.6 %collective-permute-start.7 = (bf16[128,1792]{1,0:T(8,128)(2,1)S(1)}, bf16[128,1792]{1,0:T(8,128)(2,1)S(1)}, u32[]{:S(2)}, u32[]{:S(2)}) collective-permute-start(bf16[128,1792]{1,0:T(8,128)(2,1)S(1)} %get-tuple-element.60), channel_id=1, source_target_pairs={{0,2},{1,3},{2,0},{3,1},{4,6},{5,7},{6,4},{7,5},{8,10},{9,11},{10,... | collective-permute-start | bytes 1376264 | tf_op jit(solution)/shard_map/ppermute | solution.py:20
  206.5 19.4 %collective-permute-start.15 = (bf16[128,1792]{1,0:T(8,128)(2,1)S(1)}, bf16[128,1792]{1,0:T(8,128)(2,1)S(1)}, u32[]{:S(2)}, u32[]{:S(2)}) collective-permute-start(bf16[128,1792]{1,0:T(8,128)(2,1)S(1)} %get-tuple-element.63), channel_id=1, source_target_pairs={{0,4},{1,5},{2,6},{3,7},{4,0},{5,1},{6,2},{7,3},{8,12},{9,13},{10,... | collective-permute-start | bytes 1376264 | tf_op jit(solution)/shard_map/ppermute | solution.py:20
  207.1 23.7 %collective-permute-start.16 = (bf16[128,1792]{1,0:T(8,128)(2,1)S(1)}, bf16[128,1792]{1,0:T(8,128)(2,1)S(1)}, u32[]{:S(2)}, u32[]{:S(2)}) collective-permute-start(bf16[128,1792]{1,0:T(8,128)(2,1)S(1)} %get-tuple-element.64), channel_id=1, source_target_pairs={{0,4},{1,5},{2,6},{3,7},{4,0},{5,1},{6,2},{7,3},{8,12},{9,13},{10,... | collective-permute-start | bytes 1376264 | tf_op jit(solution)/shard_map/ppermute | solution.py:20
  211.2 24.6 %collective-permute-start.53 = (bf16[64,1792]{1,0:T(8,128)(2,1)S(1)}, bf16[64,1792]{1,0:T(8,128)(2,1)S(1)}, u32[]{:S(2)}, u32[]{:S(2)}) collective-permute-start(bf16[64,1792]{1,0:T(8,128)(2,1)S(1)} %add_convert_fusion.42), channel_id=1, source_target_pairs={{0,4},{1,5},{2,6},{3,7},{4,0},{5,1},{6,2},{7,3},{8,12},{9,13},{10,... | collective-permute-start | bytes 688136 | tf_op jit(solution)/shard_map/ppermute | solution.py:20
  216.4 24.3 %collective-permute-start.54 = (bf16[64,1792]{1,0:T(8,128)(2,1)S(1)}, bf16[64,1792]{1,0:T(8,128)(2,1)S(1)}, u32[]{:S(2)}, u32[]{:S(2)}) collective-permute-start(bf16[64,1792]{1,0:T(8,128)(2,1)S(1)} %add_convert_fusion.41), channel_id=1, source_target_pairs={{0,4},{1,5},{2,6},{3,7},{4,0},{5,1},{6,2},{7,3},{8,12},{9,13},{10,... | collective-permute-start | bytes 688136 | tf_op jit(solution)/shard_map/ppermute | solution.py:20
  225.3 83.5 %collective-permute-start.59 = (bf16[64,1792]{1,0:T(8,128)(2,1)S(1)}, bf16[64,1792]{1,0:T(8,128)(2,1)S(1)}, u32[]{:S(2)}, u32[]{:S(2)}) collective-permute-start(bf16[64,1792]{1,0:T(8,128)(2,1)S(1)} %add_convert_fusion.38), channel_id=1, source_target_pairs={{0,2},{1,3},{2,0},{3,1},{4,6},{5,7},{6,4},{7,5},{8,10},{9,11},{10,... | collective-permute-start | bytes 688136 | tf_op jit(solution)/shard_map/ppermute | solution.py:20
  225.9 84.4 %collective-permute-start.60 = (bf16[64,1792]{1,0:T(8,128)(2,1)S(1)}, bf16[64,1792]{1,0:T(8,128)(2,1)S(1)}, u32[]{:S(2)}, u32[]{:S(2)}) collective-permute-start(bf16[64,1792]{1,0:T(8,128)(2,1)S(1)} %add_convert_fusion.37), channel_id=1, source_target_pairs={{0,2},{1,3},{2,0},{3,1},{4,6},{5,7},{6,4},{7,5},{8,10},{9,11},{10,... | collective-permute-start | bytes 688136 | tf_op jit(solution)/shard_map/ppermute | solution.py:20
  230.8 14.7 %collective-permute-start.39 = (bf16[64,1792]{1,0:T(8,128)(2,1)S(1)}, bf16[64,1792]{1,0:T(8,128)(2,1)S(1)}, u32[]{:S(2)}, u32[]{:S(2)}) collective-permute-start(bf16[64,1792]{1,0:T(8,128)(2,1)S(1)} %add_convert_fusion.50), channel_id=1, source_target_pairs={{0,4},{1,5},{2,6},{3,7},{4,0},{5,1},{6,2},{7,3},{8,12},{9,13},{10,... | collective-permute-start | bytes 688136 | tf_op jit(solution)/shard_map/ppermute | solution.py:20
  235.7 14.7 %collective-permute-start.40 = (bf16[64,1792]{1,0:T(8,128)(2,1)S(1)}, bf16[64,1792]{1,0:T(8,128)(2,1)S(1)}, u32[]{:S(2)}, u32[]{:S(2)}) collective-permute-start(bf16[64,1792]{1,0:T(8,128)(2,1)S(1)} %add_convert_fusion.49), channel_id=1, source_target_pairs={{0,4},{1,5},{2,6},{3,7},{4,0},{5,1},{6,2},{7,3},{8,12},{9,13},{10,... | collective-permute-start | bytes 688136 | tf_op jit(solution)/shard_map/ppermute | solution.py:20
  240.6 88.7 %collective-permute-start.45 = (bf16[64,1792]{1,0:T(8,128)(2,1)S(1)}, bf16[64,1792]{1,0:T(8,128)(2,1)S(1)}, u32[]{:S(2)}, u32[]{:S(2)}) collective-permute-start(bf16[64,1792]{1,0:T(8,128)(2,1)S(1)} %add_convert_fusion.46), channel_id=1, source_target_pairs={{0,2},{1,3},{2,0},{3,1},{4,6},{5,7},{6,4},{7,5},{8,10},{9,11},{10,... | collective-permute-start | bytes 688136 | tf_op jit(solution)/shard_map/ppermute | solution.py:20
  245.6 9.8 %collective-permute-start.25 = (bf16[64,1792]{1,0:T(8,128)(2,1)S(1)}, bf16[64,1792]{1,0:T(8,128)(2,1)S(1)}, u32[]{:S(2)}, u32[]{:S(2)}) collective-permute-start(bf16[64,1792]{1,0:T(8,128)(2,1)S(1)} %add_convert_fusion.58), channel_id=1, source_target_pairs={{0,4},{1,5},{2,6},{3,7},{4,0},{5,1},{6,2},{7,3},{8,12},{9,13},{10,... | collective-permute-start | bytes 688136 | tf_op jit(solution)/shard_map/ppermute | solution.py:20
  250.5 9.8 %collective-permute-start.26 = (bf16[64,1792]{1,0:T(8,128)(2,1)S(1)}, bf16[64,1792]{1,0:T(8,128)(2,1)S(1)}, u32[]{:S(2)}, u32[]{:S(2)}) collective-permute-start(bf16[64,1792]{1,0:T(8,128)(2,1)S(1)} %add_convert_fusion.57), channel_id=1, source_target_pairs={{0,4},{1,5},{2,6},{3,7},{4,0},{5,1},{6,2},{7,3},{8,12},{9,13},{10,... | collective-permute-start | bytes 688136 | tf_op jit(solution)/shard_map/ppermute | solution.py:20
  255.4 9.8 %collective-permute-start.8 = (bf16[64,1792]{1,0:T(8,128)(2,1)S(1)}, bf16[64,1792]{1,0:T(8,128)(2,1)S(1)}, u32[]{:S(2)}, u32[]{:S(2)}) collective-permute-start(bf16[64,1792]{1,0:T(8,128)(2,1)S(1)} %add_convert_fusion.66), channel_id=1, source_target_pairs={{0,4},{1,5},{2,6},{3,7},{4,0},{5,1},{6,2},{7,3},{8,12},{9,13},{10,... | collective-permute-start | bytes 688136 | tf_op jit(solution)/shard_map/ppermute | solution.py:20
  265.2 65.7 %collective-permute-start.46 = (bf16[64,1792]{1,0:T(8,128)(2,1)S(1)}, bf16[64,1792]{1,0:T(8,128)(2,1)S(1)}, u32[]{:S(2)}, u32[]{:S(2)}) collective-permute-start(bf16[64,1792]{1,0:T(8,128)(2,1)S(1)} %add_convert_fusion.45), channel_id=1, source_target_pairs={{0,2},{1,3},{2,0},{3,1},{4,6},{5,7},{6,4},{7,5},{8,10},{9,11},{10,... | collective-permute-start | bytes 688136 | tf_op jit(solution)/shard_map/ppermute | solution.py:20
  295.6 12.6 %collective-permute-start.56 = (bf16[128,1792]{1,0:T(8,128)(2,1)S(1)}, bf16[128,1792]{1,0:T(8,128)(2,1)S(1)}, u32[]{:S(2)}, u32[]{:S(2)}) collective-permute-start(bf16[128,1792]{1,0:T(8,128)(2,1)S(1)} %pad_maximum_fusion.7), channel_id=1, source_target_pairs={{0,2},{1,3},{2,0},{3,1},{4,6},{5,7},{6,4},{7,5},{8,10},{9,11},{10,... | collective-permute-start | bytes 1376264 | tf_op jit(solution)/shard_map/ppermute | solution.py:20
  308.2 41.6 %collective-permute-start.31 = (bf16[64,1792]{1,0:T(8,128)(2,1)S(1)}, bf16[64,1792]{1,0:T(8,128)(2,1)S(1)}, u32[]{:S(2)}, u32[]{:S(2)}) collective-permute-start(bf16[64,1792]{1,0:T(8,128)(2,1)S(1)} %add_convert_fusion.54), channel_id=1, source_target_pairs={{0,2},{1,3},{2,0},{3,1},{4,6},{5,7},{6,4},{7,5},{8,10},{9,11},{10,... | collective-permute-start | bytes 688136 | tf_op jit(solution)/shard_map/ppermute | solution.py:20
  308.8 42.6 %collective-permute-start.32 = (bf16[64,1792]{1,0:T(8,128)(2,1)S(1)}, bf16[64,1792]{1,0:T(8,128)(2,1)S(1)}, u32[]{:S(2)}, u32[]{:S(2)}) collective-permute-start(bf16[64,1792]{1,0:T(8,128)(2,1)S(1)} %add_convert_fusion.53), channel_id=1, source_target_pairs={{0,2},{1,3},{2,0},{3,1},{4,6},{5,7},{6,4},{7,5},{8,10},{9,11},{10,... | collective-permute-start | bytes 688136 | tf_op jit(solution)/shard_map/ppermute | solution.py:20
  310.4 18.4 %collective-permute-start.42 = (bf16[128,1792]{1,0:T(8,128)(2,1)S(1)}, bf16[128,1792]{1,0:T(8,128)(2,1)S(1)}, u32[]{:S(2)}, u32[]{:S(2)}) collective-permute-start(bf16[128,1792]{1,0:T(8,128)(2,1)S(1)} %pad_maximum_fusion.5), channel_id=1, source_target_pairs={{0,2},{1,3},{2,0},{3,1},{4,6},{5,7},{6,4},{7,5},{8,10},{9,11},{10,... | collective-permute-start | bytes 1376264 | tf_op jit(solution)/shard_map/ppermute | solution.py:20
  328.7 34.5 %collective-permute-start.17 = (bf16[64,1792]{1,0:T(8,128)(2,1)S(1)}, bf16[64,1792]{1,0:T(8,128)(2,1)S(1)}, u32[]{:S(2)}, u32[]{:S(2)}) collective-permute-start(bf16[64,1792]{1,0:T(8,128)(2,1)S(1)} %add_convert_fusion.62), channel_id=1, source_target_pairs={{0,2},{1,3},{2,0},{3,1},{4,6},{5,7},{6,4},{7,5},{8,10},{9,11},{10,... | collective-permute-start | bytes 688136 | tf_op jit(solution)/shard_map/ppermute | solution.py:20
  329.3 33.9 %collective-permute-start.18 = (bf16[64,1792]{1,0:T(8,128)(2,1)S(1)}, bf16[64,1792]{1,0:T(8,128)(2,1)S(1)}, u32[]{:S(2)}, u32[]{:S(2)}) collective-permute-start(bf16[64,1792]{1,0:T(8,128)(2,1)S(1)} %add_convert_fusion.61), channel_id=1, source_target_pairs={{0,2},{1,3},{2,0},{3,1},{4,6},{5,7},{6,4},{7,5},{8,10},{9,11},{10,... | collective-permute-start | bytes 688136 | tf_op jit(solution)/shard_map/ppermute | solution.py:20
  330.9 18.4 %collective-permute-start.28 = (bf16[128,1792]{1,0:T(8,128)(2,1)S(1)}, bf16[128,1792]{1,0:T(8,128)(2,1)S(1)}, u32[]{:S(2)}, u32[]{:S(2)}) collective-permute-start(bf16[128,1792]{1,0:T(8,128)(2,1)S(1)} %pad_maximum_fusion.3), channel_id=1, source_target_pairs={{0,2},{1,3},{2,0},{3,1},{4,6},{5,7},{6,4},{7,5},{8,10},{9,11},{10,... | collective-permute-start | bytes 1376264 | tf_op jit(solution)/shard_map/ppermute | solution.py:20
  349.2 13.4 %collective-permute-start.14 = (bf16[128,1792]{1,0:T(8,128)(2,1)S(1)}, bf16[128,1792]{1,0:T(8,128)(2,1)S(1)}, u32[]{:S(2)}, u32[]{:S(2)}) collective-permute-start(bf16[128,1792]{1,0:T(8,128)(2,1)S(1)} %pad_maximum_fusion.1), channel_id=1, source_target_pairs={{0,2},{1,3},{2,0},{3,1},{4,6},{5,7},{6,4},{7,5},{8,10},{9,11},{10,... | collective-permute-start | bytes 1376264 | tf_op jit(solution)/shard_map/ppermute | solution.py:20
  349.8 15.6 %collective-permute-start.61 = (bf16[64,1792]{1,0:T(8,128)(2,1)S(1)}, bf16[64,1792]{1,0:T(8,128)(2,1)S(1)}, u32[]{:S(2)}, u32[]{:S(2)}) collective-permute-start(bf16[64,1792]{1,0:T(8,128)(2,1)S(1)} %get-tuple-element.118), channel_id=1, source_target_pairs={{0,2},{1,3},{2,0},{3,1},{4,6},{5,7},{6,4},{7,5},{8,10},{9,11},{10,... | collective-permute-start | bytes 688136 | tf_op jit(solution)/shard_map/ppermute | solution.py:20
  351.4 16.6 %collective-permute-start.47 = (bf16[64,1792]{1,0:T(8,128)(2,1)S(1)}, bf16[64,1792]{1,0:T(8,128)(2,1)S(1)}, u32[]{:S(2)}, u32[]{:S(2)}) collective-permute-start(bf16[64,1792]{1,0:T(8,128)(2,1)S(1)} %get-tuple-element.114), channel_id=1, source_target_pairs={{0,2},{1,3},{2,0},{3,1},{4,6},{5,7},{6,4},{7,5},{8,10},{9,11},{10,... | collective-permute-start | bytes 688136 | tf_op jit(solution)/shard_map/ppermute | solution.py:20
  363.5 9.3 %collective-permute-start.19 = (bf16[64,1792]{1,0:T(8,128)(2,1)S(1)}, bf16[64,1792]{1,0:T(8,128)(2,1)S(1)}, u32[]{:S(2)}, u32[]{:S(2)}) collective-permute-start(bf16[64,1792]{1,0:T(8,128)(2,1)S(1)} %get-tuple-element.110), channel_id=1, source_target_pairs={{0,2},{1,3},{2,0},{3,1},{4,6},{5,7},{6,4},{7,5},{8,10},{9,11},{10,... | collective-permute-start | bytes 688136 | tf_op jit(solution)/shard_map/ppermute | solution.py:20
  365.5 12.3 %collective-permute-start.62 = (bf16[128,1792]{1,0:T(8,128)(2,1)S(1)}, bf16[128,1792]{1,0:T(8,128)(2,1)S(1)}, u32[]{:S(2)}, u32[]{:S(2)}) collective-permute-start(bf16[128,1792]{1,0:T(8,128)(2,1)S(1)} %pad_maximum_fusion.8), channel_id=1, source_target_pairs={{0,4},{1,5},{2,6},{3,7},{4,0},{5,1},{6,2},{7,3},{8,12},{9,13},{10,... | collective-permute-start | bytes 1376264 | tf_op jit(solution)/shard_map/ppermute | solution.py:20
  368.0 14.8 %collective-permute-start.48 = (bf16[128,1792]{1,0:T(8,128)(2,1)S(1)}, bf16[128,1792]{1,0:T(8,128)(2,1)S(1)}, u32[]{:S(2)}, u32[]{:S(2)}) collective-permute-start(bf16[128,1792]{1,0:T(8,128)(2,1)S(1)} %pad_maximum_fusion.6), channel_id=1, source_target_pairs={{0,4},{1,5},{2,6},{3,7},{4,0},{5,1},{6,2},{7,3},{8,12},{9,13},{10,... | collective-permute-start | bytes 1376264 | tf_op jit(solution)/shard_map/ppermute | solution.py:20
  370.4 17.2 %collective-permute-start.34 = (bf16[128,1792]{1,0:T(8,128)(2,1)S(1)}, bf16[128,1792]{1,0:T(8,128)(2,1)S(1)}, u32[]{:S(2)}, u32[]{:S(2)}) collective-permute-start(bf16[128,1792]{1,0:T(8,128)(2,1)S(1)} %pad_maximum_fusion.4), channel_id=1, source_target_pairs={{0,4},{1,5},{2,6},{3,7},{4,0},{5,1},{6,2},{7,3},{8,12},{9,13},{10,... | collective-permute-start | bytes 1376264 | tf_op jit(solution)/shard_map/ppermute | solution.py:20
  372.9 19.7 %collective-permute-start.20 = (bf16[128,1792]{1,0:T(8,128)(2,1)S(1)}, bf16[128,1792]{1,0:T(8,128)(2,1)S(1)}, u32[]{:S(2)}, u32[]{:S(2)}) collective-permute-start(bf16[128,1792]{1,0:T(8,128)(2,1)S(1)} %pad_maximum_fusion.2), channel_id=1, source_target_pairs={{0,4},{1,5},{2,6},{3,7},{4,0},{5,1},{6,2},{7,3},{8,12},{9,13},{10,... | collective-permute-start | bytes 1376264 | tf_op jit(solution)/shard_map/ppermute | solution.py:20
  377.9 32.5 %collective-permute-start.66 = (bf16[512,1792]{1,0:T(8,128)(2,1)S(1)}, bf16[512,1792]{1,0:T(8,128)(2,1)S(1)}, u32[]{:S(2)}, u32[]{:S(2)}) collective-permute-start(bf16[512,1792]{1,0:T(8,128)(2,1)S(1)} %constant_dynamic-update-slice_fusion.18), channel_id=1, source_target_pairs={{0,1},{1,0},{2,3},{3,2},{4,5},{5,4},{6,7},{7,6},{8,9},{9,8},{10,11... | collective-permute-start | bytes 5505032 | tf_op jit(solution)/shard_map/ppermute | solution.py:20
  382.8 25.5 %collective-permute-start.65 = (bf16[512,1792]{1,0:T(8,128)(2,1)S(1)}, bf16[512,1792]{1,0:T(8,128)(2,1)S(1)}, u32[]{:S(2)}, u32[]{:S(2)}) collective-permute-start(bf16[512,1792]{1,0:T(8,128)(2,1)S(1)} %constant_dynamic-update-slice_fusion.12), channel_id=1, source_target_pairs={{0,1},{1,0},{2,3},{3,2},{4,5},{5,4},{6,7},{7,6},{8,9},{9,8},{10,11... | collective-permute-start | bytes 5505032 | tf_op jit(solution)/shard_map/ppermute | solution.py:20
  387.7 18.5 %collective-permute-start.64 = (bf16[512,1792]{1,0:T(8,128)(2,1)S(1)}, bf16[512,1792]{1,0:T(8,128)(2,1)S(1)}, u32[]{:S(2)}, u32[]{:S(2)}) collective-permute-start(bf16[512,1792]{1,0:T(8,128)(2,1)S(1)} %constant_dynamic-update-slice_fusion.6), channel_id=1, source_target_pairs={{0,1},{1,0},{2,3},{3,2},{4,5},{5,4},{6,7},{7,6},{8,9},{9,8},{10,11... | collective-permute-start | bytes 5505032 | tf_op jit(solution)/shard_map/ppermute | solution.py:20
  392.6 11.5 %collective-permute-start.63 = (bf16[512,1792]{1,0:T(8,128)(2,1)S(1)}, bf16[512,1792]{1,0:T(8,128)(2,1)S(1)}, u32[]{:S(2)}, u32[]{:S(2)}) collective-permute-start(bf16[512,1792]{1,0:T(8,128)(2,1)S(1)} %constant_dynamic-update-slice_fusion), channel_id=1, source_target_pairs={{0,1},{1,0},{2,3},{3,2},{4,5},{5,4},{6,7},{7,6},{8,9},{9,8},{10,11... | collective-permute-start | bytes 5505032 | tf_op jit(solution)/shard_map/ppermute | solution.py:20
  414.3 14.7 %collective-permute-start.69 = (bf16[128,1024]{1,0:T(8,128)(2,1)}, bf16[128,1024]{1,0:T(8,128)(2,1)S(1)}, u32[]{:S(2)}, u32[]{:S(2)}) collective-permute-start(bf16[128,1024]{1,0:T(8,128)(2,1)} %pad_maximum_fusion.10), channel_id=1, source_target_pairs={{0,24},{8,0},{16,8},{24,16},{1,25},{9,1},{17,9},{25,17},{2,26},{10... | collective-permute-start | bytes 786440 | tf_op jit(solution)/shard_map/ppermute | solution.py:24
  416.2 13.0 %collective-permute-start.67 = (bf16[128,1024]{1,0:T(8,128)(2,1)}, bf16[128,1024]{1,0:T(8,128)(2,1)}, u32[]{:S(2)}, u32[]{:S(2)}) collective-permute-start(bf16[128,1024]{1,0:T(8,128)(2,1)} %pad_maximum_fusion.9), channel_id=1, source_target_pairs={{0,8},{8,16},{16,24},{24,0},{1,9},{9,17},{17,25},{25,1},{2,10},{10... | collective-permute-start | bytes 786440 | tf_op jit(solution)/shard_map/ppermute | solution.py:24
  429.1 29.4 %collective-permute-start.70 = (bf16[256,1024]{1,0:T(8,128)(2,1)S(1)}, bf16[256,1024]{1,0:T(8,128)(2,1)S(1)}, u32[]{:S(2)}, u32[]{:S(2)}) collective-permute-start(bf16[256,1024]{1,0:T(8,128)(2,1)S(1)} %add_convert_fusion.2), channel_id=1, source_target_pairs={{0,24},{8,0},{16,8},{24,16},{1,25},{9,1},{17,9},{25,17},{2,26},{10... | collective-permute-start | bytes 1572872 | tf_op jit(solution)/shard_map/ppermute | solution.py:24
  430.3 28.2 %collective-permute-start.68 = (bf16[256,1024]{1,0:T(8,128)(2,1)S(1)}, bf16[256,1024]{1,0:T(8,128)(2,1)S(1)}, u32[]{:S(2)}, u32[]{:S(2)}) collective-permute-start(bf16[256,1024]{1,0:T(8,128)(2,1)S(1)} %add_convert_fusion.3), channel_id=1, source_target_pairs={{0,8},{8,16},{16,24},{24,0},{1,9},{9,17},{17,25},{25,1},{2,10},{10... | collective-permute-start | bytes 1572872 | tf_op jit(solution)/shard_map/ppermute | solution.py:24
  432.3 21.6 %collective-permute-start.71 = (f32[1,1024]{1,0:T(1,128)S(1)}, f32[1,1024]{1,0:T(1,128)S(1)}, u32[]{:S(2)}, u32[]{:S(2)}) collective-permute-start(f32[1,1024]{1,0:T(1,128)S(1)} %get-tuple-element.104), channel_id=1, source_target_pairs={{0,8},{8,0},{16,24},{24,16},{1,9},{9,1},{17,25},{25,17},{2,10},{10... | collective-permute-start | bytes 12296 | tf_op jit(solution)/shard_map/ppermute | solution.py:20
  (35 other events, 592.4 us)
